TPU v7x, 256 devices: a whole 4x4x8 slice. The times are simulated.
256 devices in a mesh: wide: 16 (over y, x), narrow: 16 (over z, core).
Axes of the slice: x: 4, y: 4, z: 8, core: 2. Of those that a mesh axis runs over, the one named last changes fastest.
Arguments:
- vectors: float32 [524288, 128], P(('wide', 'narrow')), may hold values from -24 to 24
- near_blocks: bfloat16 [1024, 3, 512, 512], P(('wide', 'narrow')), may hold values from -0.15625 to 0.15625
- leaf_basis: bfloat16 [524288, 256], P(('wide', 'narrow')), may hold values from -0.125 to 0.125
- transfer: bfloat16 [256, 256, 256], P(('wide', 'narrow')), may hold values from -0.09375 to 0.09375
- leaf_coupling: bfloat16 [256, 6, 256, 256], P(('wide', 'narrow')), may hold values from -0.15625 to 0.15625
- leaf_partners: int32 [256, 6], P(('wide', 'narrow')), may hold values from 0 to 15, as said below
- parent_coupling: bfloat16 [16, 3, 256, 256], P('wide'), may hold values from -0.21875 to 0.21875
- parent_partners: int32 [16, 3], P('wide'), may hold values from 0 to 15, as said below
- shifts: float32 [128], replicated, may hold values from -1 to 1
Outputs:
- filtered: float32 [524288, 128], P(('wide', 'narrow'))
Inputs may be any that keep to these rules, and one draw needn't show every extreme that they name: `leaf_partners`: row l lists 6 different sibling indices, none equal to l mod 16. `parent_partners`: row p lists 3 different parent indices, none equal to p.
All inputs are finite; a program needn't handle non-finite values.
Results may differ from a plain program's by a relative error of at most 0.01.
Values may be sent and summed in bfloat16 or wider, within the bound.
No kernel may reach another device: no remote copies, remote signals or barrier semaphores. Data moves between devices by JAX's collectives and lax.ppermute only.
A program may use at most 64 MiB of HBM per device.

v0:
```python
import functools
import jax
import jax.numpy as jnp
from jax import lax
from jax.sharding import Mesh
from jax.sharding import PartitionSpec as P

BLK = 512
DEGREE = 3
WIDE_NARROW = ("wide_0", "wide_1", "narrow_0", "narrow_1")
NARROW = ("narrow_0", "narrow_1")
WIDE = ("wide_0", "wide_1")


def extended_2(shard, sides, width):
    edges = {}
    for axis, dim in sides:
        size, length = (lax.axis_size(axis), shard.shape[dim])
        up = [(i, (i + 1) % size) for i in range(size - 1)]
        last = lax.slice_in_dim(shard, length - width, length, axis=dim)
        leading = lax.slice_in_dim(shard, 0, width, axis=dim)
        edges[dim] = (
            lax.ppermute(last, axis, up),
            lax.ppermute(leading, axis, [(b, a) for a, b in up]),
        )
    done = []
    for _, dim in sides:
        low, high = edges[dim]
        around = [(width, width) if d in done else (0, 0) for d in range(shard.ndim)]
        shard = jnp.concatenate([jnp.pad(low, around), shard, jnp.pad(high, around)], axis=dim)
        done.append(dim)
    return shard


def whole_of(shard, axes, dim):
    out = shard
    for number in range(len(axes) - 1, -1, -1):
        out = lax.all_gather(out, axes[number], axis=dim, tiled=True)
    return out


def split_up(shard, dim, size):
    lengths = shard.shape
    pieces = shard.reshape(*lengths[:dim], size, lengths[dim] // size, *lengths[dim + 1 :])
    return jnp.moveaxis(pieces, dim, 0)


def summed_on_arrival(shard, axis, dim):
    pieces = split_up(shard, dim, lax.axis_size(axis))
    arrived = lax.all_to_all(pieces, axis, split_axis=0, concat_axis=0, tiled=True)
    return arrived.astype(jnp.float32).sum(axis=0)


def copy_for_each(shard, axis):
    copies = jnp.broadcast_to(shard, (lax.axis_size(axis), *shard.shape))
    return lax.all_to_all(copies, axis, split_axis=0, concat_axis=0, tiled=True)


def joined_along(pieces, dim):
    pieces = jnp.moveaxis(pieces, 0, dim)
    lengths = pieces.shape
    return pieces.reshape(*lengths[:dim], lengths[dim] * lengths[dim + 1], *lengths[dim + 2 :])


def gather_directly(shard, axis, dim):
    pieces = copy_for_each(shard, axis)
    return joined_along(pieces, dim)


def over_axes_2(shard, axes):
    return functools.reduce(lax.psum, axes, shard)


def pick_fold(partners, piece):
    indices = jnp.arange(piece.shape[0], dtype=jnp.int32)
    select = (partners[:, None] == indices[None, :]).astype(jnp.bfloat16)
    return jnp.einsum("jm,mrv->jrv", select, piece, preferred_element_type=jnp.float32)


def shards(
    vectors,
    near_blocks,
    leaf_basis,
    transfer,
    leaf_coupling,
    leaf_partners,
    parent_coupling,
    parent_partners,
    shifts,
):
    local_rows = vectors.shape[0]
    count_blocks = local_rows // BLK
    columns = vectors.shape[1]

    def apply_operator(field):
        vin = field.astype(jnp.bfloat16)
        extended = extended_2(vin, ((WIDE_NARROW, 0),), BLK)
        fields = extended.reshape(count_blocks + 2, BLK, columns)
        near = jnp.einsum(
            "bij,bjv->biv", near_blocks[:, 0], fields[:-2], preferred_element_type=jnp.float32
        )
        near = near + jnp.einsum(
            "bij,bjv->biv", near_blocks[:, 1], fields[1:-1], preferred_element_type=jnp.float32
        )
        near = near + jnp.einsum(
            "bij,bjv->biv", near_blocks[:, 2], fields[2:], preferred_element_type=jnp.float32
        )
        near = near.reshape(local_rows, columns)
        coeff = lax.dot_general(
            leaf_basis, vin, (((0,), (0,)), ((), ())), preferred_element_type=jnp.float32
        )
        coeff_b = coeff.astype(jnp.bfloat16)
        picked = pick_fold(leaf_partners[0], whole_of(coeff_b[None], NARROW, 0))
        leaf_far = jnp.einsum(
            "jrs,jsv->rv",
            leaf_coupling[0],
            picked.astype(jnp.bfloat16),
            preferred_element_type=jnp.float32,
        )
        upward = lax.dot_general(
            transfer[0], coeff_b, (((0,), (0,)), ((), ())), preferred_element_type=jnp.float32
        )
        share = summed_on_arrival(upward.astype(jnp.bfloat16), NARROW, 1)
        top_in = share.astype(jnp.bfloat16)[None]
        gathered = pick_fold(parent_partners[0], gather_directly(top_in, WIDE, 0))
        part_out = jnp.einsum(
            "jrs,jsv->rv",
            parent_coupling[0],
            gathered.astype(jnp.bfloat16),
            preferred_element_type=jnp.float32,
        ).astype(jnp.bfloat16)
        parent_out = lax.all_gather(part_out, NARROW, axis=1, tiled=True)
        downward = jnp.dot(transfer[0], parent_out, preferred_element_type=jnp.float32)
        far_coeff = (leaf_far + downward).astype(jnp.bfloat16)
        return near + jnp.dot(leaf_basis, far_coeff, preferred_element_type=jnp.float32)

    previous = vectors
    current = apply_operator(vectors) - shifts[None, :] * vectors
    for step in range(1, DEGREE):
        following = 2.0 * (apply_operator(current) - shifts[None, :] * current) - previous
        previous, current = (current, following)
    squares = over_axes_2(jnp.sum(current * current, axis=0), WIDE_NARROW)
    total_rows = local_rows * lax.axis_size(WIDE) * lax.axis_size(NARROW)
    meansq = squares / total_rows
    return current / jnp.sqrt(meansq + 1e-06)[None, :]


def solution(mesh):
    finer = Mesh(mesh.devices.reshape(4, 4, 8, 2), ("wide_0", "wide_1", "narrow_0", "narrow_1"))
    placed = (
        P(WIDE_NARROW, None),
        P(WIDE_NARROW, None, None, None),
        P(WIDE_NARROW, None),
        P(WIDE_NARROW, None, None),
        P(WIDE_NARROW, None, None, None),
        P(WIDE_NARROW, None),
        P(WIDE, None, None, None),
        P(WIDE, None),
        P(),
    )
    return jax.shard_map(
        shards, mesh=finer, in_specs=placed, out_specs=P(WIDE_NARROW, None), check_vma=False
    )
```

profile of v0, /device:TPU:1, one launch (start us, length us, event | category | flops | bytes accessed | tf_op | source)
XLA Modules:
  0.0 249.5 jit_solution(17678883639465677823)
XLA Ops:
  6.5 1.4 convert_element_type.102
  8.1 0.5 convolution_convert_fusion.5
  8.6 1.7 fusion.70
  10.3 10.0 %all-to-all-start = ((bf16[16,256,8]{1,2,0:T(8,128)(2,1)}), bf16[16,256,8]{1,2,0:T(8,128)(2,1)S(1)}, u32[]{:S(2)}, u32[]{:S(2)}) async-start(bf16[16,256,8]{1,2,0:T(8,128)(2,1)} %fusion.70), calls=%async_computation | async-start | bytes 131072 | tf_op jit(solution)/shard_map/all_to_all | solution.py:50
  20.3 2.0 all-gather
  22.4 3.5 %collective-permute-start = (bf16[512,128]{1,0:T(8,128)(2,1)S(1)}, bf16[512,128]{1,0:T(8,128)(2,1)S(1)}, u32[]{:S(2)}, u32[]{:S(2)}) collective-permute-start(bf16[512,128]{1,0:T(8,128)(2,1)S(1)} %get-tuple-element.15), channel_id=1, source_target_pairs={{0,1},{1,2},{2,3},{3,4},{4,5},{5,6},{6,7},{7,8},{8,9},{9,10},{10,1... | collective-permute-start | bytes 393224 | tf_op jit(solution)/shard_map/ppermute | solution.py:23
  25.9 1.9 collective-permute-start.1
  27.9 3.4 %fusion.20 = f32[4,512,128]{1,2,0:T(8,128)} fusion(bf16[4,512,128]{2,1,0:T(8,128)(2,1)S(1)} %bitcast.247, bf16[4,3,512,512]{3,2,1,0:T(8,128)(2,1)} %param.10), kind=kOutput, calls=%fused_computation.23 | convolution fusion | flops 268435456 | bytes 3670016 | tf_op jit(solution)/shard_map/bij,bjv->biv/dot_general | solution.py:102
  31.3 1.6 copy.56
  32.9 0.6 broadcast_in_dim.13
  33.5 6.8 %all-to-all-start.1 = ((bf16[16,1,256,8]{2,3,1,0:T(8,128)(2,1)}), bf16[16,1,256,8]{2,3,1,0:T(8,128)(2,1)S(1)}, u32[]{:S(2)}, u32[]{:S(2)}) async-start(bf16[16,1,256,8]{2,3,1,0:T(8,128)(2,1)} %broadcast_in_dim.13), calls=%async_computation.1 | async-start | bytes 131072 | tf_op jit(solution)/shard_map/all_to_all | solution.py:56
  40.4 2.5 %fusion.40 = f32[4,512,128]{1,2,0:T(8,128)S(1)} fusion(bf16[4,512,128]{2,1,0:T(8,128)(2,1)S(1)} %bitcast.251, bf16[4,3,512,512]{3,2,1,0:T(8,128)(2,1)} %param.10), kind=kOutput, calls=%fused_computation.41 | convolution fusion | flops 268435456 | bytes 3670016 | tf_op jit(solution)/shard_map/bij,bjv->biv/dot_general | solution.py:105
  42.9 3.7 %fusion.46 = f32[4,512,128]{1,2,0:T(8,128)} fusion(f32[4,512,128]{1,2,0:T(8,128)S(1)} %fusion.40, f32[4,512,128]{1,2,0:T(8,128)} %fusion.20, bf16[4,512,128]{2,1,0:T(8,128)(2,1)S(1)} %bitcast.254, bf16[4,3,512,512]{3,2,1,0:T(8,128)(2,1)} %param.10), kind=kOutput, calls=%fused_computation.43 | convolution fusion | flops 268959744 | bytes 5767168 | tf_op jit(solution)/shard_map/bij,bjv->biv/dot_general | solution.py:99
  46.7 2.5 %copy.50 = f32[4,512,128]{2,1,0:T(8,128)} copy(f32[4,512,128]{1,2,0:T(8,128)} %fusion.46) | data formatting | bytes 2097152 | tf_op jit(solution)/shard_map/add | solution.py:105
  49.2 2.5 %copy.55 = f32[2048,128]{0,1:T(8,128)} copy(f32[2048,128]{1,0:T(8,128)} %bitcast.249) | data formatting | bytes 2097152 | tf_op jit(solution)/shard_map/reshape | solution.py:108
  52.1 19.2 %all_gather.29 = bf16[256,128]{0,1:T(8,128)(2,1)} all-gather(bf16[256,8]{0,1:T(8,128)(2,1)S(1)} %fusion.78), channel_id=1, replica_groups=mesh['wide_0'=4,'wide_1'=4,'narrow_0'=8,'narrow_1'=2] {'narrow_0','narro..., dimensions={1}, use_global_device_ids=true | all-gather | bytes 69632 | tf_op jit(solution)/shard_map/all_gather | solution.py:132
  71.3 1.9 convolution_convert_fusion.2
  73.2 1.1 convolution_bitcast_fusion.5
  74.3 3.0 %fusion.135 = (bf16[2048,128]{0,1:T(8,128)(2,1)S(1)}, f32[2048,128]{0,1:T(8,128)}) fusion(f32[2048,128]{0,1:T(8,128)S(1)} %copy.56, f32[128]{0:T(128)S(1)} %copy-done.8, f32[2048,128]{0,1:T(8,128)} %copy.55, bf16[2048,256]{1,0:T(8,128)(2,1)S(1)} %copy-done, f32[128,256]{1,0:T(8,128)} %convolution_bitcast_fusion.5, bf16[256,128]{0,1:T(8,128)(2,1)} %all_gather.29, ...), kind=kOutput, calls=%fused_computation.141 | convolution fusion | flops 152109056 | bytes 5046784 | tf_op jit(solution)/shard_map/dot_general | solution.py:135
  77.6 0.6 copy-done.6
  78.2 0.8 fusion.71
  79.0 6.0 %all-to-all-start.2 = ((bf16[16,256,8]{1,2,0:T(8,128)(2,1)}), bf16[16,256,8]{1,2,0:T(8,128)(2,1)}, u32[]{:S(2)}, u32[]{:S(2)}) async-start(bf16[16,256,8]{1,2,0:T(8,128)(2,1)} %fusion.71), calls=%async_computation.2 | async-start | bytes 131072 | tf_op jit(solution)/shard_map/all_to_all | solution.py:50
  85.0 3.4 %all-gather.1 = bf16[512,128]{0,1:T(8,128)(2,1)} all-gather(bf16[256,128]{0,1:T(8,128)(2,1)} %bitcast.257), channel_id=3, replica_groups=mesh['wide_0'=4,'wide_1'=4,'narrow_0'=8,'narrow_1'=2] {'narrow_1'}, dimensions={0}, use_global_device_ids=true | all-gather | bytes 196608 | tf_op jit(solution)/shard_map/all_gather | solution.py:38
  88.3 1.7 copy.80
  90.0 0.7 fusion.133
  90.8 3.5 %collective-permute-start.2 = (bf16[512,128]{0,1:T(8,128)(2,1)}, bf16[512,128]{0,1:T(8,128)(2,1)}, u32[]{:S(2)}, u32[]{:S(2)}) collective-permute-start(bf16[512,128]{0,1:T(8,128)(2,1)} %get-tuple-element.11), channel_id=1, source_target_pairs={{0,1},{1,2},{2,3},{3,4},{4,5},{5,6},{6,7},{7,8},{8,9},{9,10},{10,1... | collective-permute-start | bytes 393224 | tf_op jit(solution)/shard_map/ppermute | solution.py:23
  94.3 1.9 collective-permute-start.3
  96.2 3.4 %fusion.18 = f32[4,128,512]{2,1,0:T(8,128)} fusion(bf16[4,3,512,512]{3,2,1,0:T(8,128)(2,1)} %param.10, bf16[16,4,8,512]{3,2,1,0:T(8,128)(2,1)S(1)} %bitcast.246), kind=kOutput, calls=%fused_computation.21 | convolution fusion | flops 268435456 | bytes 3670016 | tf_op jit(solution)/shard_map/bij,bjv->biv/dot_general | solution.py:102
  99.6 0.9 reduce_sum.46
  100.5 0.6 broadcast_in_dim.15
  101.1 7.0 %all-to-all-start.3 = ((bf16[16,1,256,8]{2,3,1,0:T(8,128)(2,1)}), bf16[16,1,256,8]{2,3,1,0:T(8,128)(2,1)}, u32[]{:S(2)}, u32[]{:S(2)}) async-start(bf16[16,1,256,8]{2,3,1,0:T(8,128)(2,1)} %broadcast_in_dim.15), calls=%async_computation.3 | async-start | bytes 131072 | tf_op jit(solution)/shard_map/all_to_all | solution.py:56
  108.1 1.1 pad_maximum_fusion.3
  109.2 2.5 fusion.12
  111.7 2.7 %fusion.55 = f32[4,16,8,512]{3,2,1,0:T(8,128)S(1)} fusion(f32[4,128,512]{2,1,0:T(8,128)S(1)} %fusion.12, f32[4,128,512]{2,1,0:T(8,128)} %fusion.18, bf16[4,3,512,512]{3,2,1,0:T(8,128)(2,1)} %param.10, bf16[16,4,8,512]{3,2,1,0:T(8,128)(2,1)S(1)} %bitcast.255), kind=kOutput, calls=%fused_computation.46 | convolution fusion | flops 268959744 | bytes 5767168 | tf_op jit(solution)/shard_map/bij,bjv->biv/dot_general | solution.py:99
  114.4 1.0 copy.91
  115.4 1.0 convolution_convert_fusion.10
  116.7 19.6 %all_gather.32 = bf16[256,128]{0,1:T(8,128)(2,1)} all-gather(bf16[256,8]{0,1:T(8,128)(2,1)S(1)} %fusion.77), channel_id=1, replica_groups=mesh['wide_0'=4,'wide_1'=4,'narrow_0'=8,'narrow_1'=2] {'narrow_0','narro..., dimensions={1}, use_global_device_ids=true | all-gather | bytes 69632 | tf_op jit(solution)/shard_map/all_gather | solution.py:132
  136.2 1.9 convolution_convert_fusion.1
  138.1 1.1 convolution_bitcast_fusion.4
  139.2 3.3 %fusion.138 = (bf16[2048,128]{0,1:T(8,128)(2,1)S(1)}, f32[2048,128]{0,1:T(8,128)}) fusion(f32[2048,128]{0,1:T(8,128)S(1)} %copy.56, f32[2048,128]{0,1:T(8,128)} %get-tuple-element.18, f32[128]{0:T(128)S(1)} %copy-done.8, f32[2048,128]{0,1:T(8,128)} %bitcast.248, bf16[2048,256]{1,0:T(8,128)(2,1)S(1)} %copy-done, f32[128,256]{1,0:T(8,128)} %convolution_bitcast_fusion.4, ...), kind=kOutput, calls=%fused_computation.142 | convolution fusion | flops 152633344 | bytes 6095360 | tf_op jit(solution)/shard_map/dot_general | solution.py:135
  142.8 0.8 fusion.72
  143.6 5.9 %all-to-all-start.4 = ((bf16[16,256,8]{1,2,0:T(8,128)(2,1)}), bf16[16,256,8]{1,2,0:T(8,128)(2,1)S(1)}, u32[]{:S(2)}, u32[]{:S(2)}) async-start(bf16[16,256,8]{1,2,0:T(8,128)(2,1)} %fusion.72), calls=%async_computation.4 | async-start | bytes 131072 | tf_op jit(solution)/shard_map/all_to_all | solution.py:50
  149.6 1.9 all-gather.2
  151.5 0.8 copy.81
  152.3 3.5 %collective-permute-start.4 = (bf16[512,128]{0,1:T(8,128)(2,1)S(1)}, bf16[512,128]{0,1:T(8,128)(2,1)S(1)}, u32[]{:S(2)}, u32[]{:S(2)}) collective-permute-start(bf16[512,128]{0,1:T(8,128)(2,1)S(1)} %get-tuple-element.7), channel_id=1, source_target_pairs={{0,1},{1,2},{2,3},{3,4},{4,5},{5,6},{6,7},{7,8},{8,9},{9,10},{10,1... | collective-permute-start | bytes 393224 | tf_op jit(solution)/shard_map/ppermute | solution.py:23
  155.9 1.9 collective-permute-start.5
  157.8 3.4 %fusion.16 = f32[4,128,512]{2,1,0:T(8,128)} fusion(bf16[4,3,512,512]{3,2,1,0:T(8,128)(2,1)} %param.10, bf16[16,4,8,512]{3,2,1,0:T(8,128)(2,1)S(1)} %bitcast.245), kind=kOutput, calls=%fused_computation.19 | convolution fusion | flops 268435456 | bytes 3670016 | tf_op jit(solution)/shard_map/bij,bjv->biv/dot_general | solution.py:102
  161.2 0.6 broadcast_in_dim.17
  161.8 6.5 %all-to-all-start.5 = ((bf16[16,1,256,8]{2,3,1,0:T(8,128)(2,1)}), bf16[16,1,256,8]{2,3,1,0:T(8,128)(2,1)}, u32[]{:S(2)}, u32[]{:S(2)}) async-start(bf16[16,1,256,8]{2,3,1,0:T(8,128)(2,1)} %broadcast_in_dim.17), calls=%async_computation.5 | async-start | bytes 131072 | tf_op jit(solution)/shard_map/all_to_all | solution.py:56
  168.5 2.4 fusion.10
  170.9 2.8 %fusion.64 = f32[4,16,8,512]{3,2,1,0:T(8,128)S(1)} fusion(f32[4,128,512]{2,1,0:T(8,128)S(1)} %fusion.10, f32[4,128,512]{2,1,0:T(8,128)} %fusion.16, bf16[4,3,512,512]{3,2,1,0:T(8,128)(2,1)} %param.10, bf16[16,4,8,512]{3,2,1,0:T(8,128)(2,1)S(1)} %bitcast.256), kind=kOutput, calls=%fused_computation.49 | convolution fusion | flops 268959744 | bytes 5767168 | tf_op jit(solution)/shard_map/bij,bjv->biv/dot_general | solution.py:99
  173.8 1.1 copy.92
  174.9 1.0 convolution_convert_fusion.9
  176.0 1.2 fusion.76
  177.1 19.0 %all_gather.35 = bf16[256,128]{0,1:T(8,128)(2,1)S(1)} all-gather(bf16[256,8]{0,1:T(8,128)(2,1)S(1)} %fusion.76), channel_id=1, replica_groups=mesh['wide_0'=4,'wide_1'=4,'narrow_0'=8,'narrow_1'=2] {'narrow_0','narro..., dimensions={1}, use_global_device_ids=true | all-gather | bytes 69632 | tf_op jit(solution)/shard_map/all_gather | solution.py:132
  196.1 1.9 convolution_convert_fusion
  198.0 0.4 convolution_bitcast_fusion.3
  198.5 3.2 %multiply_reduce_fusion = (f32[128]{0:T(128)S(1)}, f32[2048,128]{0,1:T(8,128)}) fusion(f32[2048,128]{0,1:T(8,128)S(1)} %copy-done.1, f32[2048,128]{0,1:T(8,128)} %get-tuple-element.20, f32[128]{0:T(128)S(1)} %copy-done.8, f32[2048,128]{0,1:T(8,128)} %bitcast.250, bf16[2048,256]{1,0:T(8,128)(2,1)S(1)} %copy-done, ...), kind=kOutput, calls=%fused_computation.86 | convolution fusion | flops 152895360 | bytes 5571584 | tf_op jit(solution)/shard_map/dot_general | solution.py:135
  201.6 7.4 %psum.28 = f32[128]{0:T(128)S(1)} all-reduce(f32[128]{0:T(128)S(1)} %get-tuple-element.21), channel_id=1, replica_groups=mesh['wide_0'=4,'wide_1'=4,'narrow_0'=8,'narrow_1'=2] {'wide_0'}, use_global_device_ids=true, to_apply=%region_4.5 | all-reduce | flops 128 | bytes 1024 | tf_op jit(solution)/shard_map/psum | solution.py:71
  209.1 8.4 %psum.29 = f32[128]{0:T(128)S(1)} all-reduce(f32[128]{0:T(128)S(1)} %psum.28), channel_id=1, replica_groups=mesh['wide_0'=4,'wide_1'=4,'narrow_0'=8,'narrow_1'=2] {'wide_1'}, use_global_device_ids=true, to_apply=%region_5.6 | all-reduce | flops 128 | bytes 1024 | tf_op jit(solution)/shard_map/psum | solution.py:71
  217.4 13.1 %psum.30 = f32[128]{0:T(128)S(1)} all-reduce(f32[128]{0:T(128)S(1)} %psum.29), channel_id=1, replica_groups=mesh['wide_0'=4,'wide_1'=4,'narrow_0'=8,'narrow_1'=2] {'narrow_0'}, use_global_device_ids=true, to_apply=%region_6.7 | all-reduce | flops 128 | bytes 1024 | tf_op jit(solution)/shard_map/psum | solution.py:71
  230.5 9.8 %psum.31 = f32[128]{0:T(128)S(1)} all-reduce(f32[128]{0:T(128)S(1)} %psum.30), channel_id=1, replica_groups=mesh['wide_0'=4,'wide_1'=4,'narrow_0'=8,'narrow_1'=2] {'narrow_1'}, use_global_device_ids=true, to_apply=%region_7.8 | all-reduce | flops 128 | bytes 1024 | tf_op jit(solution)/shard_map/psum | solution.py:71
  240.3 1.4 broadcast_divide_fusion
  241.7 1.3 copy.76
  (52 shorter events, 2.0 us)
Async XLA Ops:
  6.5 1.5 copy-start
  10.3 22.5 %all-to-all-start = ((bf16[16,256,8]{1,2,0:T(8,128)(2,1)}), bf16[16,256,8]{1,2,0:T(8,128)(2,1)S(1)}, u32[]{:S(2)}, u32[]{:S(2)}) async-start(bf16[16,256,8]{1,2,0:T(8,128)(2,1)} %fusion.70), calls=%async_computation | async-start | bytes 131072 | tf_op jit(solution)/shard_map/all_to_all | solution.py:50
  20.3 51.0 %all-gather.7.cloned.1.call-start = ((), (), s32[]{:S(2)}) async-start(), calls=%async_computation.6 | async-start | bytes 1179648 | tf_op jit(solution)/shard_map/all_gather | solution.py:38
  22.4 17.9 %collective-permute-start = (bf16[512,128]{1,0:T(8,128)(2,1)S(1)}, bf16[512,128]{1,0:T(8,128)(2,1)S(1)}, u32[]{:S(2)}, u32[]{:S(2)}) collective-permute-start(bf16[512,128]{1,0:T(8,128)(2,1)S(1)} %get-tuple-element.15), channel_id=1, source_target_pairs={{0,1},{1,2},{2,3},{3,4},{4,5},{5,6},{6,7},{7,8},{8,9},{9,10},{10,1... | collective-permute-start | bytes 393224 | tf_op jit(solution)/shard_map/ppermute | solution.py:23
  25.9 14.3 %collective-permute-start.1 = (bf16[512,128]{1,0:T(8,128)(2,1)S(1)}, bf16[512,128]{1,0:T(8,128)(2,1)S(1)}, u32[]{:S(2)}, u32[]{:S(2)}) collective-permute-start(bf16[512,128]{1,0:T(8,128)(2,1)S(1)} %get-tuple-element.16), channel_id=1, source_target_pairs={{1,0},{2,1},{3,2},{4,3},{5,4},{6,5},{7,6},{8,7},{9,8},{10,9},{11,1... | collective-permute-start | bytes 393224 | tf_op jit(solution)/shard_map/ppermute | solution.py:24
  33.5 18.3 %all-to-all-start.1 = ((bf16[16,1,256,8]{2,3,1,0:T(8,128)(2,1)}), bf16[16,1,256,8]{2,3,1,0:T(8,128)(2,1)S(1)}, u32[]{:S(2)}, u32[]{:S(2)}) async-start(bf16[16,1,256,8]{2,3,1,0:T(8,128)(2,1)} %broadcast_in_dim.13), calls=%async_computation.1 | async-start | bytes 131072 | tf_op jit(solution)/shard_map/all_to_all | solution.py:56
  40.3 11.4 %copy-start.9 = (s32[1,3]{1,0:T(1,128)S(1)}, s32[1,3]{1,0:T(1,128)}, u32[]{:S(2)}) copy-start(s32[1,3]{1,0:T(1,128)} %param.16) | copy-start | bytes 40
  40.3 11.6 %copy-start.4 = (bf16[1,3,256,256]{3,2,1,0:T(8,128)(2,1)S(1)}, bf16[1,3,256,256]{3,2,1,0:T(8,128)(2,1)}, u32[]{:S(2)}) copy-start(bf16[1,3,256,256]{3,2,1,0:T(8,128)(2,1)} %param.15) | copy-start | bytes 1179652
  40.4 30.9 %copy-start.7 = (s32[1,6]{1,0:T(1,128)S(1)}, s32[1,6]{1,0:T(1,128)}, u32[]{:S(2)}) copy-start(s32[1,6]{1,0:T(1,128)} %param.14) | copy-start | bytes 76
  42.9 30.3 %copy-start.2 = (bf16[1,6,256,256]{3,2,1,0:T(8,128)(2,1)S(1)}, bf16[1,6,256,256]{3,2,1,0:T(8,128)(2,1)}, u32[]{:S(2)}) copy-start(bf16[1,6,256,256]{3,2,1,0:T(8,128)(2,1)} %param.13) | copy-start | bytes 2359300
  42.9 31.4 %copy-start.3 = (bf16[1,256,256]{2,1,0:T(8,128)(2,1)S(1)}, bf16[1,256,256]{2,1,0:T(8,128)(2,1)}, u32[]{:S(2)}) copy-start(bf16[1,256,256]{2,1,0:T(8,128)(2,1)} %param.12) | copy-start | bytes 393220
  42.9 31.4 %copy-start.8 = (f32[128]{0:T(128)S(1)}, f32[128]{0:T(128)}, u32[]{:S(2)}) copy-start(f32[128]{0:T(128)} %param.17) | copy-start | bytes 1540
  77.5 0.6 copy-start.6
  79.0 20.6 %all-to-all-start.2 = ((bf16[16,256,8]{1,2,0:T(8,128)(2,1)}), bf16[16,256,8]{1,2,0:T(8,128)(2,1)}, u32[]{:S(2)}, u32[]{:S(2)}) async-start(bf16[16,256,8]{1,2,0:T(8,128)(2,1)} %fusion.71), calls=%async_computation.2 | async-start | bytes 131072 | tf_op jit(solution)/shard_map/all_to_all | solution.py:50
  84.9 51.3 %all-gather.9.cloned.1.call-start = ((), (), s32[]{:S(2)}) async-start(), calls=%async_computation.7 | async-start | bytes 1179648 | tf_op jit(solution)/shard_map/all_gather | solution.py:38
  90.8 17.3 %collective-permute-start.2 = (bf16[512,128]{0,1:T(8,128)(2,1)}, bf16[512,128]{0,1:T(8,128)(2,1)}, u32[]{:S(2)}, u32[]{:S(2)}) collective-permute-start(bf16[512,128]{0,1:T(8,128)(2,1)} %get-tuple-element.11), channel_id=1, source_target_pairs={{0,1},{1,2},{2,3},{3,4},{4,5},{5,6},{6,7},{7,8},{8,9},{9,10},{10,1... | collective-permute-start | bytes 393224 | tf_op jit(solution)/shard_map/ppermute | solution.py:23
  94.3 13.8 %collective-permute-start.3 = (bf16[512,128]{0,1:T(8,128)(2,1)}, bf16[512,128]{0,1:T(8,128)(2,1)}, u32[]{:S(2)}, u32[]{:S(2)}) collective-permute-start(bf16[512,128]{0,1:T(8,128)(2,1)} %get-tuple-element.12), channel_id=1, source_target_pairs={{1,0},{2,1},{3,2},{4,3},{5,4},{6,5},{7,6},{8,7},{9,8},{10,9},{11,1... | collective-permute-start | bytes 393224 | tf_op jit(solution)/shard_map/ppermute | solution.py:24
  101.1 14.3 %all-to-all-start.3 = ((bf16[16,1,256,8]{2,3,1,0:T(8,128)(2,1)}), bf16[16,1,256,8]{2,3,1,0:T(8,128)(2,1)}, u32[]{:S(2)}, u32[]{:S(2)}) async-start(bf16[16,1,256,8]{2,3,1,0:T(8,128)(2,1)} %broadcast_in_dim.15), calls=%async_computation.3 | async-start | bytes 131072 | tf_op jit(solution)/shard_map/all_to_all | solution.py:56
  109.2 7.3 %copy-start.5 = (bf16[1,3,256,256]{3,2,1,0:T(8,128)(2,1)S(1)}, bf16[1,3,256,256]{3,2,1,0:T(8,128)(2,1)}, u32[]{:S(2)}) copy-start(bf16[1,3,256,256]{3,2,1,0:T(8,128)(2,1)} %param.15) | copy-start | bytes 1179652
  143.6 17.6 %all-to-all-start.4 = ((bf16[16,256,8]{1,2,0:T(8,128)(2,1)}), bf16[16,256,8]{1,2,0:T(8,128)(2,1)S(1)}, u32[]{:S(2)}, u32[]{:S(2)}) async-start(bf16[16,256,8]{1,2,0:T(8,128)(2,1)} %fusion.72), calls=%async_computation.4 | async-start | bytes 131072 | tf_op jit(solution)/shard_map/all_to_all | solution.py:50
  149.6 46.6 %all-gather.11.cloned.1.call-start = ((), (), s32[]{:S(2)}) async-start(), calls=%async_computation.8 | async-start | bytes 1179648 | tf_op jit(solution)/shard_map/all_gather | solution.py:38
  152.3 16.1 %collective-permute-start.4 = (bf16[512,128]{0,1:T(8,128)(2,1)S(1)}, bf16[512,128]{0,1:T(8,128)(2,1)S(1)}, u32[]{:S(2)}, u32[]{:S(2)}) collective-permute-start(bf16[512,128]{0,1:T(8,128)(2,1)S(1)} %get-tuple-element.7), channel_id=1, source_target_pairs={{0,1},{1,2},{2,3},{3,4},{4,5},{5,6},{6,7},{7,8},{8,9},{9,10},{10,1... | collective-permute-start | bytes 393224 | tf_op jit(solution)/shard_map/ppermute | solution.py:23
  155.9 12.5 %collective-permute-start.5 = (bf16[512,128]{0,1:T(8,128)(2,1)S(1)}, bf16[512,128]{0,1:T(8,128)(2,1)S(1)}, u32[]{:S(2)}, u32[]{:S(2)}) collective-permute-start(bf16[512,128]{0,1:T(8,128)(2,1)S(1)} %get-tuple-element.8), channel_id=1, source_target_pairs={{1,0},{2,1},{3,2},{4,3},{5,4},{6,5},{7,6},{8,7},{9,8},{10,9},{11,1... | collective-permute-start | bytes 393224 | tf_op jit(solution)/shard_map/ppermute | solution.py:24
  161.8 13.1 %all-to-all-start.5 = ((bf16[16,1,256,8]{2,3,1,0:T(8,128)(2,1)}), bf16[16,1,256,8]{2,3,1,0:T(8,128)(2,1)}, u32[]{:S(2)}, u32[]{:S(2)}) async-start(bf16[16,1,256,8]{2,3,1,0:T(8,128)(2,1)} %broadcast_in_dim.17), calls=%async_computation.5 | async-start | bytes 131072 | tf_op jit(solution)/shard_map/all_to_all | solution.py:56
  170.9 27.5 %copy-start.1 = (f32[2048,128]{0,1:T(8,128)S(1)}, f32[2048,128]{0,1:T(8,128)}, u32[]{:S(2)}) copy-start(f32[2048,128]{0,1:T(8,128)} %get-tuple-element.18) | copy-start | bytes 3145732
Sparse Core Ops, SparseCore 0:
  22.9 35.2 all-gather.6
  90.2 34.5 all-gather.8
  152.4 34.1 all-gather.10
where the time goes:
time: 251 us; the launch traced here: 250 us
  blocking collectives  104 us (41%)
  starting transfers between devices  58.6 us (23%)
  matrix products  52.7 us (21%)
  local copies, waits for them, and re-layouts  15.9 us (6%)
  between operations  13.5 us (5%)
  other arithmetic  4.89 us (2%)
    all_gather x3, blocking collectives, apply_operator(): parent_out = lax.all_gather(part_out, NARROW, axis=1, tiled=True)  57.7 us
    psum x4, blocking collectives, over_axes_2(): return functools.reduce(lax.psum, axes, shard)  38.6 us
    all_to_all x3, starting transfers between devices, summed_on_arrival(): lax.all_to_all(pieces, axis, split_axis=0, concat_axis=0, tiled=True)  21.9 us
    all_to_all x3, starting transfers between devices, copy_for_each(): return lax.all_to_all(copies, axis, split_axis=0, concat_axis=0, tiled=True)  20.3 us
    ppermute x3, starting transfers between devices, extended_2(): lax.ppermute(last, axis, up)  10.6 us
    dot_general x3, matrix products, apply_operator(): jnp.einsum('bij,bjv->biv', near_blocks[:, 1], fields[1:-1], preferred_ele...  10.2 us
    dot_general x3, matrix products, apply_operator(): jnp.dot(leaf_basis, far_coeff, preferred_element_type=jnp.float32)  9.46 us
    dot_general x3, matrix products, apply_operator(): jnp.einsum('bij,bjv->biv', near_blocks[:, 0], fields[:-2], preferred_elem...  9.28 us
  transfers between devices with their start and end apart: 15, of which 1 were waited for; matrix products, arithmetic and copies ran while one was open for 19% of the time, Pallas kernels for 0%

commit v1 on v0

--- a/solution.py
+++ b/solution.py
@@ -129,7 +129,9 @@
             gathered.astype(jnp.bfloat16),
             preferred_element_type=jnp.float32,
         ).astype(jnp.bfloat16)
-        parent_out = lax.all_gather(part_out, NARROW, axis=1, tiled=True)
+        parent_out = jnp.concatenate(
+            lax.all_to_all(jnp.stack([part_out] * lax.axis_size(NARROW)), NARROW, 0, 0), axis=1
+        )
         downward = jnp.dot(transfer[0], parent_out, preferred_element_type=jnp.float32)
         far_coeff = (leaf_far + downward).astype(jnp.bfloat16)
         return near + jnp.dot(leaf_basis, far_coeff, preferred_element_type=jnp.float32)

time: 251 us -> 234 us (0.932)
  blocking collectives: 104 us -> 45 us
  starting transfers between devices: 58.6 us -> 82.2 us
  waiting for transfers between devices: 0.21 us -> 15.4 us
  local copies, waits for them, and re-layouts: 15.9 us -> 18.6 us
    all_gather x3 -> x0, blocking collectives: 57.7 us -> none  [apply_operator(): parent_out = lax.all_gather(part_out, NARROW, axis=1, tiled=True)]
    all_to_all x0 -> x3, starting transfers between devices: none -> 28 us  [apply_operator(): lax.all_to_all(jnp.stack([part_out] * lax.axis_size(NARROW)), NARROW, 0, 0)]
    all_to_all x0 -> x3, waiting for transfers between devices: none -> 15.1 us  [apply_operator(): lax.all_to_all(jnp.stack([part_out] * lax.axis_size(NARROW)), NARROW, 0, 0)]
    all_to_all x3, starting transfers between devices: 21.9 us -> 17.4 us  [summed_on_arrival(): lax.all_to_all(pieces, axis, split_axis=0, concat_axis=0, tiled=True)]
  transfers between devices with their start and end apart: 15 -> 18, of which waited for: 1 -> 4; matrix products, arithmetic and copies ran while one was open for 19% -> 24% of each run, Pallas kernels for 0% -> 0%
where the time goes in v1:
time: 234 us; the launch traced here: 232 us
  starting transfers between devices  82.2 us (35%)
  matrix products  52.6 us (22%)
  blocking collectives  45 us (19%)
  local copies, waits for them, and re-layouts  18.6 us (8%)
  waiting for transfers between devices  15.4 us (7%)
  between operations  13.5 us (6%)
  other arithmetic  4.9 us (2%)
    psum x4, blocking collectives, over_axes_2(): return functools.reduce(lax.psum, axes, shard)  37.7 us
    all_to_all x3, starting transfers between devices, apply_operator(): lax.all_to_all(jnp.stack([part_out] * lax.axis_size(NARROW)), NARROW, 0, 0)  28 us
    all_to_all x3, starting transfers between devices, copy_for_each(): return lax.all_to_all(copies, axis, split_axis=0, concat_axis=0, tiled=True)  20.4 us
    all_to_all x3, starting transfers between devices, summed_on_arrival(): lax.all_to_all(pieces, axis, split_axis=0, concat_axis=0, tiled=True)  17.4 us
    all_to_all x3, waiting for transfers between devices, apply_operator(): lax.all_to_all(jnp.stack([part_out] * lax.axis_size(NARROW)), NARROW, 0, 0)  15.1 us
    ppermute x3, starting transfers between devices, extended_2(): lax.ppermute(last, axis, up)  10.5 us
    dot_general x3, matrix products, apply_operator(): jnp.einsum('bij,bjv->biv', near_blocks[:, 1], fields[1:-1], preferred_ele...  10.1 us
    dot_general x3, matrix products, apply_operator(): jnp.dot(leaf_basis, far_coeff, preferred_element_type=jnp.float32)  9.44 us
  transfers between devices with their start and end apart: 18, of which 4 were waited for; matrix products, arithmetic and copies ran while one was open for 24% of the time, Pallas kernels for 0%

profile of v1, /device:TPU:1, one launch (start us, length us, event | category | flops | bytes accessed | tf_op | source)
XLA Modules:
  0.0 232.2 jit_solution(4796229621980294444)
XLA Ops:
  6.5 1.4 convert_element_type.102
  8.6 1.7 fusion.70
  10.3 10.0 %all-to-all-start = ((bf16[16,256,8]{1,2,0:T(8,128)(2,1)}), bf16[16,256,8]{1,2,0:T(8,128)(2,1)S(1)}, u32[]{:S(2)}, u32[]{:S(2)}) async-start(bf16[16,256,8]{1,2,0:T(8,128)(2,1)} %fusion.70), calls=%async_computation | async-start | bytes 131072 | tf_op jit(solution)/shard_map/all_to_all | solution.py:50
  20.3 2.0 all-gather
  22.4 3.5 %collective-permute-start = (bf16[512,128]{1,0:T(8,128)(2,1)S(1)}, bf16[512,128]{1,0:T(8,128)(2,1)S(1)}, u32[]{:S(2)}, u32[]{:S(2)}) collective-permute-start(bf16[512,128]{1,0:T(8,128)(2,1)S(1)} %get-tuple-element.15), channel_id=1, source_target_pairs={{0,1},{1,2},{2,3},{3,4},{4,5},{5,6},{6,7},{7,8},{8,9},{9,10},{10,1... | collective-permute-start | bytes 393224 | tf_op jit(solution)/shard_map/ppermute | solution.py:23
  25.9 1.9 collective-permute-start.1
  27.9 3.4 %fusion.20 = f32[4,512,128]{1,2,0:T(8,128)} fusion(bf16[4,512,128]{2,1,0:T(8,128)(2,1)S(1)} %bitcast.268, bf16[4,3,512,512]{3,2,1,0:T(8,128)(2,1)} %param.10), kind=kOutput, calls=%fused_computation.23 | convolution fusion | flops 268435456 | bytes 3670016 | tf_op jit(solution)/shard_map/bij,bjv->biv/dot_general | solution.py:102
  31.2 1.6 copy.59
  33.5 6.8 %all-to-all-start.1 = ((bf16[16,1,256,8]{2,3,1,0:T(8,128)(2,1)}), bf16[16,1,256,8]{2,3,1,0:T(8,128)(2,1)S(1)}, u32[]{:S(2)}, u32[]{:S(2)}) async-start(bf16[16,1,256,8]{2,3,1,0:T(8,128)(2,1)} %broadcast_in_dim.13), calls=%async_computation.1 | async-start | bytes 131072 | tf_op jit(solution)/shard_map/all_to_all | solution.py:56
  40.4 2.5 %fusion.40 = f32[4,512,128]{1,2,0:T(8,128)S(1)} fusion(bf16[4,512,128]{2,1,0:T(8,128)(2,1)S(1)} %bitcast.272, bf16[4,3,512,512]{3,2,1,0:T(8,128)(2,1)} %param.10), kind=kOutput, calls=%fused_computation.41 | convolution fusion | flops 268435456 | bytes 3670016 | tf_op jit(solution)/shard_map/bij,bjv->biv/dot_general | solution.py:105
  42.9 3.8 %fusion.46 = f32[4,512,128]{1,2,0:T(8,128)} fusion(f32[4,512,128]{1,2,0:T(8,128)S(1)} %fusion.40, f32[4,512,128]{1,2,0:T(8,128)} %fusion.20, bf16[4,512,128]{2,1,0:T(8,128)(2,1)S(1)} %bitcast.275, bf16[4,3,512,512]{3,2,1,0:T(8,128)(2,1)} %param.10), kind=kOutput, calls=%fused_computation.43 | convolution fusion | flops 268959744 | bytes 5767168 | tf_op jit(solution)/shard_map/bij,bjv->biv/dot_general | solution.py:99
  46.7 2.5 %copy.53 = f32[4,512,128]{2,1,0:T(8,128)} copy(f32[4,512,128]{1,2,0:T(8,128)} %fusion.46) | data formatting | bytes 2097152 | tf_op jit(solution)/shard_map/add | solution.py:105
  49.2 2.5 %copy.58 = f32[2048,128]{0,1:T(8,128)} copy(f32[2048,128]{1,0:T(8,128)} %bitcast.270) | data formatting | bytes 2097152 | tf_op jit(solution)/shard_map/reshape | solution.py:108
  52.1 0.7 stack.6
  52.8 8.8 %all-to-all-start.2 = ((bf16[16,256,8]{1,2,0:T(8,128)(2,1)}), bf16[16,256,8]{1,2,0:T(8,128)(2,1)}, u32[]{:S(2)}, u32[]{:S(2)}) async-start(bf16[16,256,8]{1,2,0:T(8,128)(2,1)} %stack.6), calls=%async_computation.2 | async-start | bytes 131072 | tf_op jit(solution)/shard_map/all_to_all | solution.py:133
  61.7 1.9 convolution_convert_fusion.2
  63.6 1.1 convolution_bitcast_fusion.5
  64.6 4.9 %all-to-all-done.2 = bf16[16,256,8]{1,2,0:T(8,128)(2,1)} async-done(((bf16[16,256,8]{1,2,0:T(8,128)(2,1)}), bf16[16,256,8]{1,2,0:T(8,128)(2,1)}, u32[]{:S(2)}, u32[]{:S(2)}) %all-to-all-start.2) | async-done | bytes 65568 | tf_op jit(solution)/shard_map/all_to_all | solution.py:133
  69.5 3.0 %fusion.141 = (bf16[2048,128]{0,1:T(8,128)(2,1)S(1)}, f32[2048,128]{0,1:T(8,128)}) fusion(f32[2048,128]{0,1:T(8,128)S(1)} %copy.59, f32[128]{0:T(128)S(1)} %copy-done.9, f32[2048,128]{0,1:T(8,128)} %copy.58, bf16[2048,256]{1,0:T(8,128)(2,1)S(1)} %copy-done, f32[128,256]{1,0:T(8,128)} %convolution_bitcast_fusion.5, bf16[1,256,256]{2,1,0:T(8,128)(2,1)S(1)} %copy-done.3, ...), kind=kOutput, calls=%fused_computation.144 | convolution fusion | flops 152109056 | bytes 5046784 | tf_op jit(solution)/shard_map/dot_general | solution.py:137
  73.4 0.8 fusion.71
  74.2 4.0 %all-to-all-start.3 = ((bf16[16,256,8]{1,2,0:T(8,128)(2,1)}), bf16[16,256,8]{1,2,0:T(8,128)(2,1)}, u32[]{:S(2)}, u32[]{:S(2)}) async-start(bf16[16,256,8]{1,2,0:T(8,128)(2,1)} %fusion.71), calls=%async_computation.3 | async-start | bytes 131072 | tf_op jit(solution)/shard_map/all_to_all | solution.py:50
  78.3 3.4 %all-gather.1 = bf16[512,128]{0,1:T(8,128)(2,1)} all-gather(bf16[256,128]{0,1:T(8,128)(2,1)} %bitcast.278), channel_id=3, replica_groups=mesh['wide_0'=4,'wide_1'=4,'narrow_0'=8,'narrow_1'=2] {'narrow_1'}, dimensions={0}, use_global_device_ids=true | all-gather | bytes 196608 | tf_op jit(solution)/shard_map/all_gather | solution.py:38
  81.7 1.6 copy.83
  83.4 0.7 fusion.139
  84.1 3.4 %collective-permute-start.2 = (bf16[512,128]{0,1:T(8,128)(2,1)}, bf16[512,128]{0,1:T(8,128)(2,1)}, u32[]{:S(2)}, u32[]{:S(2)}) collective-permute-start(bf16[512,128]{0,1:T(8,128)(2,1)} %get-tuple-element.11), channel_id=1, source_target_pairs={{0,1},{1,2},{2,3},{3,4},{4,5},{5,6},{6,7},{7,8},{8,9},{9,10},{10,1... | collective-permute-start | bytes 393224 | tf_op jit(solution)/shard_map/ppermute | solution.py:23
  87.5 1.9 collective-permute-start.3
  89.4 3.4 %fusion.18 = f32[4,128,512]{2,1,0:T(8,128)} fusion(bf16[4,3,512,512]{3,2,1,0:T(8,128)(2,1)} %param.10, bf16[16,4,8,512]{3,2,1,0:T(8,128)(2,1)S(1)} %bitcast.267), kind=kOutput, calls=%fused_computation.21 | convolution fusion | flops 268435456 | bytes 3670016 | tf_op jit(solution)/shard_map/bij,bjv->biv/dot_general | solution.py:102
  92.8 0.9 reduce_sum.46
  94.3 7.0 %all-to-all-start.4 = ((bf16[16,1,256,8]{2,3,1,0:T(8,128)(2,1)}), bf16[16,1,256,8]{2,3,1,0:T(8,128)(2,1)}, u32[]{:S(2)}, u32[]{:S(2)}) async-start(bf16[16,1,256,8]{2,3,1,0:T(8,128)(2,1)} %broadcast_in_dim.15), calls=%async_computation.4 | async-start | bytes 131072 | tf_op jit(solution)/shard_map/all_to_all | solution.py:56
  101.3 1.1 pad_maximum_fusion.3
  102.4 2.5 %fusion.12 = f32[4,128,512]{2,1,0:T(8,128)S(1)} fusion(bf16[4,3,512,512]{3,2,1,0:T(8,128)(2,1)} %param.10, bf16[16,4,8,512]{3,2,1,0:T(8,128)(2,1)S(1)} %bitcast.273), kind=kOutput, calls=%fused_computation.15 | convolution fusion | flops 268435456 | bytes 3670016 | tf_op jit(solution)/shard_map/bij,bjv->biv/dot_general | solution.py:105
  104.9 2.7 %fusion.55 = f32[4,16,8,512]{3,2,1,0:T(8,128)S(1)} fusion(f32[4,128,512]{2,1,0:T(8,128)S(1)} %fusion.12, f32[4,128,512]{2,1,0:T(8,128)} %fusion.18, bf16[4,3,512,512]{3,2,1,0:T(8,128)(2,1)} %param.10, bf16[16,4,8,512]{3,2,1,0:T(8,128)(2,1)S(1)} %bitcast.276), kind=kOutput, calls=%fused_computation.46 | convolution fusion | flops 268959744 | bytes 5767168 | tf_op jit(solution)/shard_map/bij,bjv->biv/dot_general | solution.py:99
  107.6 1.0 copy.94
  108.6 1.0 convolution_convert_fusion.10
  109.9 0.7 stack.7
  110.6 9.2 %all-to-all-start.5 = ((bf16[16,256,8]{1,2,0:T(8,128)(2,1)}), bf16[16,256,8]{1,2,0:T(8,128)(2,1)S(1)}, u32[]{:S(2)}, u32[]{:S(2)}) async-start(bf16[16,256,8]{1,2,0:T(8,128)(2,1)} %stack.7), calls=%async_computation.5 | async-start | bytes 131072 | tf_op jit(solution)/shard_map/all_to_all | solution.py:133
  119.8 1.9 convolution_convert_fusion.1
  121.7 1.1 convolution_bitcast_fusion.4
  122.8 4.8 %all-to-all-done.5 = bf16[16,256,8]{1,2,0:T(8,128)(2,1)S(1)} async-done(((bf16[16,256,8]{1,2,0:T(8,128)(2,1)}), bf16[16,256,8]{1,2,0:T(8,128)(2,1)S(1)}, u32[]{:S(2)}, u32[]{:S(2)}) %all-to-all-start.5) | async-done | bytes 65568 | tf_op jit(solution)/shard_map/all_to_all | solution.py:133
  128.2 3.3 %fusion.146 = (bf16[2048,128]{0,1:T(8,128)(2,1)S(1)}, f32[2048,128]{0,1:T(8,128)}) fusion(f32[2048,128]{0,1:T(8,128)S(1)} %copy.59, f32[2048,128]{0,1:T(8,128)} %get-tuple-element.18, f32[128]{0:T(128)S(1)} %copy-done.9, f32[2048,128]{0,1:T(8,128)} %bitcast.269, bf16[2048,256]{1,0:T(8,128)(2,1)S(1)} %copy-done, f32[128,256]{1,0:T(8,128)} %convolution_bitcast_fusion.4, ...), kind=kOutput, calls=%fused_computation.145 | convolution fusion | flops 152633344 | bytes 6095360 | tf_op jit(solution)/shard_map/dot_general | solution.py:137
  131.8 0.8 fusion.72
  132.6 3.4 %all-to-all-start.6 = ((bf16[16,256,8]{1,2,0:T(8,128)(2,1)}), bf16[16,256,8]{1,2,0:T(8,128)(2,1)S(1)}, u32[]{:S(2)}, u32[]{:S(2)}) async-start(bf16[16,256,8]{1,2,0:T(8,128)(2,1)} %fusion.72), calls=%async_computation.6 | async-start | bytes 131072 | tf_op jit(solution)/shard_map/all_to_all | solution.py:50
  136.0 1.9 all-gather.2
  137.9 0.7 copy.84
  138.7 3.5 %collective-permute-start.4 = (bf16[512,128]{0,1:T(8,128)(2,1)S(1)}, bf16[512,128]{0,1:T(8,128)(2,1)S(1)}, u32[]{:S(2)}, u32[]{:S(2)}) collective-permute-start(bf16[512,128]{0,1:T(8,128)(2,1)S(1)} %get-tuple-element.7), channel_id=1, source_target_pairs={{0,1},{1,2},{2,3},{3,4},{4,5},{5,6},{6,7},{7,8},{8,9},{9,10},{10,1... | collective-permute-start | bytes 393224 | tf_op jit(solution)/shard_map/ppermute | solution.py:23
  142.3 1.9 collective-permute-start.5
  144.2 3.4 %fusion.16 = f32[4,128,512]{2,1,0:T(8,128)} fusion(bf16[4,3,512,512]{3,2,1,0:T(8,128)(2,1)} %param.10, bf16[16,4,8,512]{3,2,1,0:T(8,128)(2,1)S(1)} %bitcast.266), kind=kOutput, calls=%fused_computation.19 | convolution fusion | flops 268435456 | bytes 3670016 | tf_op jit(solution)/shard_map/bij,bjv->biv/dot_general | solution.py:102
  148.3 6.6 %all-to-all-start.7 = ((bf16[16,1,256,8]{2,3,1,0:T(8,128)(2,1)}), bf16[16,1,256,8]{2,3,1,0:T(8,128)(2,1)}, u32[]{:S(2)}, u32[]{:S(2)}) async-start(bf16[16,1,256,8]{2,3,1,0:T(8,128)(2,1)} %broadcast_in_dim.17), calls=%async_computation.7 | async-start | bytes 131072 | tf_op jit(solution)/shard_map/all_to_all | solution.py:56
  155.0 2.4 %fusion.10 = f32[4,128,512]{2,1,0:T(8,128)S(1)} fusion(bf16[4,3,512,512]{3,2,1,0:T(8,128)(2,1)} %param.10, bf16[16,4,8,512]{3,2,1,0:T(8,128)(2,1)S(1)} %bitcast.274), kind=kOutput, calls=%fused_computation.13 | convolution fusion | flops 268435456 | bytes 3670016 | tf_op jit(solution)/shard_map/bij,bjv->biv/dot_general | solution.py:105
  157.5 2.8 %fusion.64 = f32[4,16,8,512]{3,2,1,0:T(8,128)S(1)} fusion(f32[4,128,512]{2,1,0:T(8,128)S(1)} %fusion.10, f32[4,128,512]{2,1,0:T(8,128)} %fusion.16, bf16[4,3,512,512]{3,2,1,0:T(8,128)(2,1)} %param.10, bf16[16,4,8,512]{3,2,1,0:T(8,128)(2,1)S(1)} %bitcast.277), kind=kOutput, calls=%fused_computation.49 | convolution fusion | flops 268959744 | bytes 5767168 | tf_op jit(solution)/shard_map/bij,bjv->biv/dot_general | solution.py:99
  160.3 1.1 copy.95
  161.5 1.0 convolution_convert_fusion.9
  162.5 1.2 fusion.76
  163.7 0.7 stack.8
  164.4 10.0 %all-to-all-start.8 = ((bf16[16,256,8]{1,2,0:T(8,128)(2,1)}), bf16[16,256,8]{1,2,0:T(8,128)(2,1)S(1)}, u32[]{:S(2)}, u32[]{:S(2)}) async-start(bf16[16,256,8]{1,2,0:T(8,128)(2,1)} %stack.8), calls=%async_computation.8 | async-start | bytes 131072 | tf_op jit(solution)/shard_map/all_to_all | solution.py:133
  174.4 1.9 convolution_convert_fusion
  176.7 5.4 %all-to-all-done.8 = bf16[16,256,8]{1,2,0:T(8,128)(2,1)S(1)} async-done(((bf16[16,256,8]{1,2,0:T(8,128)(2,1)}), bf16[16,256,8]{1,2,0:T(8,128)(2,1)S(1)}, u32[]{:S(2)}, u32[]{:S(2)}) %all-to-all-start.8) | async-done | bytes 65568 | tf_op jit(solution)/shard_map/all_to_all | solution.py:133
  182.1 3.2 %multiply_reduce_fusion = (f32[128]{0:T(128)S(1)}, f32[2048,128]{0,1:T(8,128)}) fusion(f32[2048,128]{0,1:T(8,128)S(1)} %copy-done.1, f32[2048,128]{0,1:T(8,128)} %get-tuple-element.20, f32[128]{0:T(128)S(1)} %copy-done.9, f32[2048,128]{0,1:T(8,128)} %bitcast.271, bf16[2048,256]{1,0:T(8,128)(2,1)S(1)} %copy-done, ...), kind=kOutput, calls=%fused_computation.86 | convolution fusion | flops 152895360 | bytes 5571584 | tf_op jit(solution)/shard_map/dot_general | solution.py:137
  185.3 7.3 %psum.28 = f32[128]{0:T(128)S(1)} all-reduce(f32[128]{0:T(128)S(1)} %get-tuple-element.21), channel_id=1, replica_groups=mesh['wide_0'=4,'wide_1'=4,'narrow_0'=8,'narrow_1'=2] {'wide_0'}, use_global_device_ids=true, to_apply=%region_4.5 | all-reduce | flops 128 | bytes 1024 | tf_op jit(solution)/shard_map/psum | solution.py:71
  192.6 8.5 %psum.29 = f32[128]{0:T(128)S(1)} all-reduce(f32[128]{0:T(128)S(1)} %psum.28), channel_id=1, replica_groups=mesh['wide_0'=4,'wide_1'=4,'narrow_0'=8,'narrow_1'=2] {'wide_1'}, use_global_device_ids=true, to_apply=%region_5.6 | all-reduce | flops 128 | bytes 1024 | tf_op jit(solution)/shard_map/psum | solution.py:71
  201.2 10.8 %psum.30 = f32[128]{0:T(128)S(1)} all-reduce(f32[128]{0:T(128)S(1)} %psum.29), channel_id=1, replica_groups=mesh['wide_0'=4,'wide_1'=4,'narrow_0'=8,'narrow_1'=2] {'narrow_0'}, use_global_device_ids=true, to_apply=%region_6.7 | all-reduce | flops 128 | bytes 1024 | tf_op jit(solution)/shard_map/psum | solution.py:71
  212.0 10.9 %psum.31 = f32[128]{0:T(128)S(1)} all-reduce(f32[128]{0:T(128)S(1)} %psum.30), channel_id=1, replica_groups=mesh['wide_0'=4,'wide_1'=4,'narrow_0'=8,'narrow_1'=2] {'narrow_1'}, use_global_device_ids=true, to_apply=%region_7.8 | all-reduce | flops 128 | bytes 1024 | tf_op jit(solution)/shard_map/psum | solution.py:71
  223.0 1.4 broadcast_divide_fusion
  224.4 1.3 copy.79
  (60 shorter events, 6.0 us)
Async XLA Ops:
  6.5 1.5 copy-start
  10.3 22.5 %all-to-all-start = ((bf16[16,256,8]{1,2,0:T(8,128)(2,1)}), bf16[16,256,8]{1,2,0:T(8,128)(2,1)S(1)}, u32[]{:S(2)}, u32[]{:S(2)}) async-start(bf16[16,256,8]{1,2,0:T(8,128)(2,1)} %fusion.70), calls=%async_computation | async-start | bytes 131072 | tf_op jit(solution)/shard_map/all_to_all | solution.py:50
  20.3 41.4 %all-gather.7.cloned.1.call-start = ((), (), s32[]{:S(2)}) async-start(), calls=%async_computation.9 | async-start | bytes 1179648 | tf_op jit(solution)/shard_map/all_gather | solution.py:38
  22.4 17.9 %collective-permute-start = (bf16[512,128]{1,0:T(8,128)(2,1)S(1)}, bf16[512,128]{1,0:T(8,128)(2,1)S(1)}, u32[]{:S(2)}, u32[]{:S(2)}) collective-permute-start(bf16[512,128]{1,0:T(8,128)(2,1)S(1)} %get-tuple-element.15), channel_id=1, source_target_pairs={{0,1},{1,2},{2,3},{3,4},{4,5},{5,6},{6,7},{7,8},{8,9},{9,10},{10,1... | collective-permute-start | bytes 393224 | tf_op jit(solution)/shard_map/ppermute | solution.py:23
  25.9 14.3 %collective-permute-start.1 = (bf16[512,128]{1,0:T(8,128)(2,1)S(1)}, bf16[512,128]{1,0:T(8,128)(2,1)S(1)}, u32[]{:S(2)}, u32[]{:S(2)}) collective-permute-start(bf16[512,128]{1,0:T(8,128)(2,1)S(1)} %get-tuple-element.16), channel_id=1, source_target_pairs={{1,0},{2,1},{3,2},{4,3},{5,4},{6,5},{7,6},{8,7},{9,8},{10,9},{11,1... | collective-permute-start | bytes 393224 | tf_op jit(solution)/shard_map/ppermute | solution.py:24
  33.5 18.2 %all-to-all-start.1 = ((bf16[16,1,256,8]{2,3,1,0:T(8,128)(2,1)}), bf16[16,1,256,8]{2,3,1,0:T(8,128)(2,1)S(1)}, u32[]{:S(2)}, u32[]{:S(2)}) async-start(bf16[16,1,256,8]{2,3,1,0:T(8,128)(2,1)} %broadcast_in_dim.13), calls=%async_computation.1 | async-start | bytes 131072 | tf_op jit(solution)/shard_map/all_to_all | solution.py:56
  40.3 11.4 %copy-start.10 = (s32[1,3]{1,0:T(1,128)S(1)}, s32[1,3]{1,0:T(1,128)}, u32[]{:S(2)}) copy-start(s32[1,3]{1,0:T(1,128)} %param.16) | copy-start | bytes 40
  40.3 11.6 %copy-start.4 = (bf16[1,3,256,256]{3,2,1,0:T(8,128)(2,1)S(1)}, bf16[1,3,256,256]{3,2,1,0:T(8,128)(2,1)}, u32[]{:S(2)}) copy-start(bf16[1,3,256,256]{3,2,1,0:T(8,128)(2,1)} %param.15) | copy-start | bytes 1179652
  40.4 21.3 %copy-start.8 = (s32[1,6]{1,0:T(1,128)S(1)}, s32[1,6]{1,0:T(1,128)}, u32[]{:S(2)}) copy-start(s32[1,6]{1,0:T(1,128)} %param.14) | copy-start | bytes 76
  42.9 20.7 %copy-start.2 = (bf16[1,6,256,256]{3,2,1,0:T(8,128)(2,1)S(1)}, bf16[1,6,256,256]{3,2,1,0:T(8,128)(2,1)}, u32[]{:S(2)}) copy-start(bf16[1,6,256,256]{3,2,1,0:T(8,128)(2,1)} %param.13) | copy-start | bytes 2359300
  42.9 26.6 %copy-start.3 = (bf16[1,256,256]{2,1,0:T(8,128)(2,1)S(1)}, bf16[1,256,256]{2,1,0:T(8,128)(2,1)}, u32[]{:S(2)}) copy-start(bf16[1,256,256]{2,1,0:T(8,128)(2,1)} %param.12) | copy-start | bytes 393220
  42.9 26.6 %copy-start.9 = (f32[128]{0:T(128)S(1)}, f32[128]{0:T(128)}, u32[]{:S(2)}) copy-start(f32[128]{0:T(128)} %param.17) | copy-start | bytes 1540
  52.8 16.7 %all-to-all-start.2 = ((bf16[16,256,8]{1,2,0:T(8,128)(2,1)}), bf16[16,256,8]{1,2,0:T(8,128)(2,1)}, u32[]{:S(2)}, u32[]{:S(2)}) async-start(bf16[16,256,8]{1,2,0:T(8,128)(2,1)} %stack.6), calls=%async_computation.2 | async-start | bytes 131072 | tf_op jit(solution)/shard_map/all_to_all | solution.py:133
  72.8 0.6 copy-start.6
  74.2 18.6 %all-to-all-start.3 = ((bf16[16,256,8]{1,2,0:T(8,128)(2,1)}), bf16[16,256,8]{1,2,0:T(8,128)(2,1)}, u32[]{:S(2)}, u32[]{:S(2)}) async-start(bf16[16,256,8]{1,2,0:T(8,128)(2,1)} %fusion.71), calls=%async_computation.3 | async-start | bytes 131072 | tf_op jit(solution)/shard_map/all_to_all | solution.py:50
  78.2 41.6 %all-gather.9.cloned.1.call-start = ((), (), s32[]{:S(2)}) async-start(), calls=%async_computation.10 | async-start | bytes 1179648 | tf_op jit(solution)/shard_map/all_gather | solution.py:38
  84.1 17.2 %collective-permute-start.2 = (bf16[512,128]{0,1:T(8,128)(2,1)}, bf16[512,128]{0,1:T(8,128)(2,1)}, u32[]{:S(2)}, u32[]{:S(2)}) collective-permute-start(bf16[512,128]{0,1:T(8,128)(2,1)} %get-tuple-element.11), channel_id=1, source_target_pairs={{0,1},{1,2},{2,3},{3,4},{4,5},{5,6},{6,7},{7,8},{8,9},{9,10},{10,1... | collective-permute-start | bytes 393224 | tf_op jit(solution)/shard_map/ppermute | solution.py:23
  87.5 13.8 %collective-permute-start.3 = (bf16[512,128]{0,1:T(8,128)(2,1)}, bf16[512,128]{0,1:T(8,128)(2,1)}, u32[]{:S(2)}, u32[]{:S(2)}) collective-permute-start(bf16[512,128]{0,1:T(8,128)(2,1)} %get-tuple-element.12), channel_id=1, source_target_pairs={{1,0},{2,1},{3,2},{4,3},{5,4},{6,5},{7,6},{8,7},{9,8},{10,9},{11,1... | collective-permute-start | bytes 393224 | tf_op jit(solution)/shard_map/ppermute | solution.py:24
  94.3 14.3 %all-to-all-start.4 = ((bf16[16,1,256,8]{2,3,1,0:T(8,128)(2,1)}), bf16[16,1,256,8]{2,3,1,0:T(8,128)(2,1)}, u32[]{:S(2)}, u32[]{:S(2)}) async-start(bf16[16,1,256,8]{2,3,1,0:T(8,128)(2,1)} %broadcast_in_dim.15), calls=%async_computation.4 | async-start | bytes 131072 | tf_op jit(solution)/shard_map/all_to_all | solution.py:56
  102.4 7.3 %copy-start.5 = (bf16[1,3,256,256]{3,2,1,0:T(8,128)(2,1)S(1)}, bf16[1,3,256,256]{3,2,1,0:T(8,128)(2,1)}, u32[]{:S(2)}) copy-start(bf16[1,3,256,256]{3,2,1,0:T(8,128)(2,1)} %param.15) | copy-start | bytes 1179652
  110.6 17.0 %all-to-all-start.5 = ((bf16[16,256,8]{1,2,0:T(8,128)(2,1)}), bf16[16,256,8]{1,2,0:T(8,128)(2,1)S(1)}, u32[]{:S(2)}, u32[]{:S(2)}) async-start(bf16[16,256,8]{1,2,0:T(8,128)(2,1)} %stack.7), calls=%async_computation.5 | async-start | bytes 131072 | tf_op jit(solution)/shard_map/all_to_all | solution.py:133
  127.6 0.6 copy-start.7
  132.6 15.0 %all-to-all-start.6 = ((bf16[16,256,8]{1,2,0:T(8,128)(2,1)}), bf16[16,256,8]{1,2,0:T(8,128)(2,1)S(1)}, u32[]{:S(2)}, u32[]{:S(2)}) async-start(bf16[16,256,8]{1,2,0:T(8,128)(2,1)} %fusion.72), calls=%async_computation.6 | async-start | bytes 131072 | tf_op jit(solution)/shard_map/all_to_all | solution.py:50
  136.0 38.3 %all-gather.11.cloned.1.call-start = ((), (), s32[]{:S(2)}) async-start(), calls=%async_computation.11 | async-start | bytes 1179648 | tf_op jit(solution)/shard_map/all_gather | solution.py:38
  138.7 16.2 %collective-permute-start.4 = (bf16[512,128]{0,1:T(8,128)(2,1)S(1)}, bf16[512,128]{0,1:T(8,128)(2,1)S(1)}, u32[]{:S(2)}, u32[]{:S(2)}) collective-permute-start(bf16[512,128]{0,1:T(8,128)(2,1)S(1)} %get-tuple-element.7), channel_id=1, source_target_pairs={{0,1},{1,2},{2,3},{3,4},{4,5},{5,6},{6,7},{7,8},{8,9},{9,10},{10,1... | collective-permute-start | bytes 393224 | tf_op jit(solution)/shard_map/ppermute | solution.py:23
  142.3 12.6 %collective-permute-start.5 = (bf16[512,128]{0,1:T(8,128)(2,1)S(1)}, bf16[512,128]{0,1:T(8,128)(2,1)S(1)}, u32[]{:S(2)}, u32[]{:S(2)}) collective-permute-start(bf16[512,128]{0,1:T(8,128)(2,1)S(1)} %get-tuple-element.8), channel_id=1, source_target_pairs={{1,0},{2,1},{3,2},{4,3},{5,4},{6,5},{7,6},{8,7},{9,8},{10,9},{11,1... | collective-permute-start | bytes 393224 | tf_op jit(solution)/shard_map/ppermute | solution.py:24
  148.3 13.2 %all-to-all-start.7 = ((bf16[16,1,256,8]{2,3,1,0:T(8,128)(2,1)}), bf16[16,1,256,8]{2,3,1,0:T(8,128)(2,1)}, u32[]{:S(2)}, u32[]{:S(2)}) async-start(bf16[16,1,256,8]{2,3,1,0:T(8,128)(2,1)} %broadcast_in_dim.17), calls=%async_computation.7 | async-start | bytes 131072 | tf_op jit(solution)/shard_map/all_to_all | solution.py:56
  157.5 24.7 %copy-start.1 = (f32[2048,128]{0,1:T(8,128)S(1)}, f32[2048,128]{0,1:T(8,128)}, u32[]{:S(2)}) copy-start(f32[2048,128]{0,1:T(8,128)} %get-tuple-element.18) | copy-start | bytes 3145732
  164.4 17.7 %all-to-all-start.8 = ((bf16[16,256,8]{1,2,0:T(8,128)(2,1)}), bf16[16,256,8]{1,2,0:T(8,128)(2,1)S(1)}, u32[]{:S(2)}, u32[]{:S(2)}) async-start(bf16[16,256,8]{1,2,0:T(8,128)(2,1)} %stack.8), calls=%async_computation.8 | async-start | bytes 131072 | tf_op jit(solution)/shard_map/all_to_all | solution.py:133
Sparse Core Ops, SparseCore 0:
  22.8 35.2 all-gather.6
  83.5 34.5 all-gather.8
  138.8 34.2 all-gather.10
